TPU v7x, 32 devices: a whole 2x2x4 slice. The times are simulated.
32 devices in a mesh: row: 4 (over y, core), col: 8 (over z, x).
Axes of the slice: x: 2, y: 2, z: 4, core: 2. Of those that a mesh axis runs over, the one named last changes fastest.
Arguments:
- root_inverse: bfloat16 [2048, 2048], P('col', 'row'), may hold values from -1 to 3, as said below
- lower_panels: bfloat16 [4, 1536, 1024], P(None, 'col', 'row'), may hold values from -0.375 to 0.375
- struct_blocks: int32 [4, 12], replicated, may hold values from 0 to 15, as said below
- struct_count: int32 [4], replicated, may hold values from 1 to 12, 32 in all
- diag_inverse: float32 [4, 1024, 1024], P(None, 'col', 'row'), may hold values from -1 to 3, as said below
Outputs:
- offdiag: bfloat16 [4, 1536, 1024], P(None, 'col', 'row')
- diag_block: float32 [4, 1024, 1024], P(None, 'col', 'row')
Inputs may be any that keep to these rules, and one draw needn't show every extreme that they name: `struct_blocks`: each row holds 12 different block numbers of the top supernode; supernode c uses the first struct_count[c] of them. `struct_count`: the counts sum to 32; the largest equals 12. `root_inverse`: Symmetric, with a dominant diagonal. `diag_inverse`: each supernode's block is symmetric; diagonal entries lie between 0.85 and 2.15, all other entries within 0.13 of zero.
All inputs are finite; a program needn't handle non-finite values.
Results may differ from a plain program's by a relative error of at most 0.0095.
Values may be sent and summed in bfloat16 or wider, within the bound.
A program may use at most 64 MiB of HBM per device.

v0:
```python
import jax
import jax.numpy as jnp
from jax import lax
from jax.sharding import PartitionSpec as P

BLOCK = 128
NSMAX = 12


def body(root_inverse, lower_panels, struct_blocks, struct_count, diag_inverse):
    col_index = lax.axis_index("col")
    root_panel = lax.all_gather(root_inverse, "row", axis=1, tiled=True)
    root_width = root_panel.shape[1]
    block_count = root_width // BLOCK
    own_rows = root_panel.shape[0]
    per_dev = own_rows // BLOCK
    local_packed = lower_panels.shape[1]

    def solve_group(lower_group, block_lists, block_counts, inverse_group):
        group_size = lower_group.shape[0]
        cols_here = lower_group.shape[2]
        gathered = lax.all_gather(lower_group, "col", axis=1, tiled=True)
        packed_total = gathered.shape[1]
        full_mask = jnp.arange(packed_total)[None, :] // BLOCK < block_counts[:, None]
        gathered = gathered * full_mask[:, :, None].astype(jnp.bfloat16)
        in_use = jnp.arange(NSMAX)[None, :] < block_counts[:, None]
        onehot = (
            (block_lists[:, None, :] == jnp.arange(block_count)[None, :, None]) & in_use[:, None, :]
        ).astype(jnp.bfloat16)
        spread = jnp.einsum(
            "gbk,gkic->gbic",
            onehot,
            gathered.reshape(group_size, NSMAX, BLOCK, cols_here),
            preferred_element_type=jnp.float32,
        )
        spread = spread.astype(jnp.bfloat16).reshape(group_size, root_width, cols_here)
        root_part = -jnp.einsum(
            "rw,gwc->grc", root_panel, spread, preferred_element_type=jnp.float32
        )
        packed_index = col_index * local_packed + jnp.arange(local_packed)
        local_mask = packed_index[None, :] // BLOCK < block_counts[:, None]
        own_select = lax.dynamic_slice_in_dim(onehot, col_index * per_dev, per_dev, 1).astype(
            jnp.float32
        )
        selected = jnp.einsum(
            "gjk,gjic->gkic",
            own_select,
            root_part.reshape(group_size, per_dev, BLOCK, cols_here),
            precision=lax.Precision.HIGHEST,
            preferred_element_type=jnp.float32,
        )
        selected = selected.reshape(group_size, packed_total, cols_here)
        offdiag = lax.psum_scatter(
            selected.astype(jnp.bfloat16), "col", scatter_dimension=1, tiled=True
        )
        full_cols = lax.all_gather(lower_group, "row", axis=2, tiled=True)
        masked_rows = full_cols * local_mask[:, :, None].astype(jnp.bfloat16)
        schur_terms = jnp.einsum(
            "gka,gkc->gac", masked_rows, offdiag, preferred_element_type=jnp.float32
        )
        schur_part = lax.psum_scatter(
            schur_terms.astype(jnp.bfloat16), "col", scatter_dimension=1, tiled=True
        ).astype(jnp.float32)
        return (offdiag, inverse_group - schur_part)

    group_size = 4
    turn_count = lower_panels.shape[0] // group_size

    def regroup(source_array):
        return source_array.reshape((turn_count, group_size) + source_array.shape[1:])

    def one_turn(running, inputs_now):
        return (running, solve_group(*inputs_now))

    finished, outputs = lax.scan(
        one_turn,
        jnp.int32(0),
        (
            regroup(lower_panels),
            regroup(struct_blocks),
            regroup(struct_count),
            regroup(diag_inverse),
        ),
    )
    offdiag_all, diag_all = outputs
    return (offdiag_all.reshape(lower_panels.shape), diag_all.reshape(diag_inverse.shape))


def solution(mesh):
    in_specs = (P("col", "row"), P(None, "col", "row"), P(), P(), P(None, "col", "row"))
    out_specs = (P(None, "col", "row"), P(None, "col", "row"))
    return jax.shard_map(body, mesh=mesh, in_specs=in_specs, out_specs=out_specs, check_vma=False)
```

profile of v0, /device:TPU:0, one launch (start us, length us, event | category | flops | bytes accessed | tf_op | source)
XLA Modules:
  0.0 269.8 jit_solution(14597254614823216027)
XLA Ops:
  7.2 0.0 all-gather.4.cloned.1.call-start
  7.2 0.7 all-gather.4.cloned.1.call-update
  7.9 0.0 all-gather.6.cloned.1.call-start
  7.9 0.7 all-gather.6.cloned.1.call-update
  8.6 0.0 all-gather.8.cloned.1.call-start
  8.7 0.7 all-gather.8.cloned.1.call-update
  9.4 0.0 reduce-scatter.3.cloned.1.call-start
  9.4 0.7 iota_compare_fusion.1
  10.2 0.7 fusion.9
  10.9 0.7 compare_convert_fusion
  11.6 0.0 copy-start.1
  11.6 61.3 %all-gather.4.cloned.1.call-done = bf16[4,1536,256]{2,1,0:T(8,128)(2,1)} async-done(((bf16[4,192,256]{2,1,0:T(8,128)(2,1)}), bf16[4,1536,256]{2,1,0:T(8,128)(2,1)}) %all-gather.4.cloned.1.call-update) | async-done | bytes 3145744 | tf_op jit(solution)/shard_map/while/body/eval_jaxpr/all_gather | solution.py:22
  72.9 2.4 broadcast_multiply_fusion
  75.3 0.0 copy-done.1
  75.3 2.0 fusion.2
  77.3 3.5 %copy.10 = bf16[4,16,128,256]{3,2,1,0:T(8,128)(2,1)} copy(bf16[4,16,128,256]{3,1,2,0:T(8,128)(2,1)S(1)} %fusion.2) | data formatting | bytes 8388608 | tf_op jit(solution)/shard_map/while/body/eval_jaxpr/convert_element_type | solution.py:36
  80.9 9.0 %all-gather.6.cloned.1.call-done = bf16[256,2048]{1,0:T(8,128)(2,1)} async-done(((bf16[256,512]{1,0:T(8,128)(2,1)}), bf16[256,2048]{1,0:T(8,128)(2,1)}) %all-gather.6.cloned.1.call-update) | async-done | bytes 1048592 | tf_op jit(solution)/shard_map/all_gather | solution.py:12
  89.9 3.8 %convolution_negate_fusion = f32[4,256,256]{1,2,0:T(8,128)S(1)} fusion(bf16[4,2048,256]{2,1,0:T(8,128)(2,1)} %bitcast.23, bf16[256,2048]{1,0:T(8,128)(2,1)} %all-gather.6.cloned.1.call-done), kind=kOutput, calls=%fused_computation.7 | convolution fusion | flops 1074003968 | bytes 6291456 | tf_op jit(solution)/shard_map/while/body/eval_jaxpr/rw,gwc->grc/dot_general | solution.py:37
  93.7 4.4 %convolution_convert_fusion = bf16[4,12,128,256]{3,1,2,0:T(8,128)(2,1)S(1)} fusion(f32[4,2,128,256]{3,2,1,0:T(8,128)S(1)} %bitcast.24, pred[4,16,12]{2,1,0:T(8,128)(4,1)S(1)} %fusion.9, s32[]{:T(128)S(6)} %select_n.26), kind=kOutput, calls=%fused_computation.3 | convolution fusion | flops 39321600 | bytes 4196356 | tf_op jit(solution)/shard_map/while/body/eval_jaxpr/gjk,gjic->gkic/dot_general | solution.py:45
  98.1 2.9 %copy.12 = bf16[4,12,128,256]{3,2,1,0:T(8,128)(2,1)} copy(bf16[4,12,128,256]{3,1,2,0:T(8,128)(2,1)S(1)} %convolution_convert_fusion) | data formatting | bytes 6291456 | tf_op jit(solution)/shard_map/while/body/eval_jaxpr/convert_element_type | solution.py:54
  101.0 0.0 copy-start.2
  101.0 0.0 reduce-scatter.3.cloned.1.call-update
  101.0 0.0 copy-start
  101.0 0.0 reduce-scatter.5.cloned.1.call-start
  101.1 0.5 copy-done.2
  101.6 0.1 compare_convert_fusion.1
  101.7 9.6 %all-gather.8.cloned.1.call-done = bf16[4,192,1024]{2,1,0:T(8,128)(2,1)} async-done(((bf16[4,192,256]{2,1,0:T(8,128)(2,1)}), bf16[4,192,1024]{2,1,0:T(8,128)(2,1)}) %all-gather.8.cloned.1.call-update) | async-done | bytes 1572880 | tf_op jit(solution)/shard_map/while/body/eval_jaxpr/all_gather | solution.py:56
  111.3 78.3 %reduce-scatter.3.cloned.1.call-done = bf16[4,192,256]{2,1,0:T(8,128)(2,1)} async-done(((bf16[4,1536,256]{2,1,0:T(8,128)(2,1)}), bf16[4,192,256]{2,1,0:T(8,128)(2,1)}) %reduce-scatter.3.cloned.1.call-update) | async-done | bytes 393232 | tf_op jit(solution)/shard_map/while/body/eval_jaxpr/reduce_scatter | solution.py:53
  189.6 3.8 %convolution_convert_fusion.1 = bf16[4,1024,256]{2,1,0:T(8,128)(2,1)} fusion(bf16[4,192,256]{2,1,0:T(8,128)(2,1)} %reduce-scatter.3.cloned.1.call-done, bf16[4,192,1024]{2,1,0:T(8,128)(2,1)} %all-gather.8.cloned.1.call-done, bf16[4,192]{1,0:T(4,128)(2,1)S(1)} %compare_convert_fusion.1), kind=kOutput, calls=%fused_computation.4 | convolution fusion | flops 404488192 | bytes 4064768 | tf_op jit(solution)/shard_map/while/body/eval_jaxpr/gka,gkc->gac/dot_general | solution.py:58
  193.4 0.0 reduce-scatter.5.cloned.1.call-update
  193.5 68.0 %reduce-scatter.5.cloned.1.call-done = bf16[4,128,256]{2,1,0:T(8,128)(2,1)} async-done(((bf16[4,1024,256]{2,1,0:T(8,128)(2,1)}), bf16[4,128,256]{2,1,0:T(8,128)(2,1)}) %reduce-scatter.5.cloned.1.call-update) | async-done | bytes 262160 | tf_op jit(solution)/shard_map/while/body/eval_jaxpr/reduce_scatter | solution.py:61
  261.5 0.0 copy-done
  261.5 1.8 convert_subtract_fusion
  (2 shorter events, 0.0 us)
Async XLA Ops:
  7.2 65.8 %all-gather.4.cloned.1.call-start = ((), (), s32[]{:S(2)}) async-start(), calls=%async_computation.2 | async-start | bytes 3538944 | tf_op jit(solution)/shard_map/while/body/eval_jaxpr/all_gather | solution.py:22
  7.9 82.0 %all-gather.6.cloned.1.call-start = ((), (), s32[]{:S(2)}) async-start(), calls=%async_computation.3 | async-start | bytes 1310720 | tf_op jit(solution)/shard_map/all_gather | solution.py:12
  8.6 102.7 %all-gather.8.cloned.1.call-start = ((), (), s32[]{:S(2)}) async-start(), calls=%async_computation.5 | async-start | bytes 1966080 | tf_op jit(solution)/shard_map/while/body/eval_jaxpr/all_gather | solution.py:56
  9.4 180.2 %reduce-scatter.3.cloned.1.call-start = ((), (), s32[]{:S(2)}) async-start(), calls=%async_computation.4 | async-start | bytes 3538944 | tf_op jit(solution)/shard_map/while/body/eval_jaxpr/reduce_scatter | solution.py:53
  11.6 63.7 %copy-start.1 = (s32[4,12]{1,0:T(4,128)S(1)}, s32[4,12]{1,0:T(4,128)}, u32[]{:S(2)}) copy-start(s32[4,12]{1,0:T(4,128)} %param.7) | copy-start | bytes 580
  101.0 0.7 copy-start.2
  101.0 160.5 %copy-start = (f32[4,128,256]{2,1,0:T(8,128)S(1)}, f32[4,128,256]{2,1,0:T(8,128)}, u32[]{:S(2)}) copy-start(f32[4,128,256]{2,1,0:T(8,128)} %param.9) | copy-start | bytes 1572868
  101.0 160.5 %reduce-scatter.5.cloned.1.call-start = ((), (), s32[]{:S(2)}) async-start(), calls=%async_computation.6 | async-start | bytes 2359296 | tf_op jit(solution)/shard_map/while/body/eval_jaxpr/reduce_scatter | solution.py:61
Sparse Core Ops, SparseCore 0:
  10.2 62.7 all-gather.3
  74.5 15.3 all-gather.5
  91.5 19.8 all-gather.7
  115.3 74.2 reduce-scatter.2
  193.6 67.8 reduce-scatter.4
where the time goes:
time: 270 us
  waiting for transfers between devices  228 us (84%)
  matrix products  14 us (5%)
  between operations  13.8 us (5%)
  local copies, waits for them, and re-layouts  6.97 us (3%)
  other arithmetic  6.43 us (2%)
    reduce_scatter x1, waiting for transfers between devices, solve_group(): lax.psum_scatter(selected.astype(jnp.bfloat16), 'col', scatter_dimension=...  78.3 us
    reduce_scatter x1, waiting for transfers between devices, solve_group(): lax.psum_scatter(schur_terms.astype(jnp.bfloat16), 'col', scatter_dimensi...  68 us
    all_gather x1, waiting for transfers between devices, solve_group(): gathered = lax.all_gather(lower_group, 'col', axis=1, tiled=True)  61.3 us
    all_gather x1, waiting for transfers between devices, solve_group(): full_cols = lax.all_gather(lower_group, 'row', axis=2, tiled=True)  9.62 us
    all_gather x1, waiting for transfers between devices, body(): root_panel = lax.all_gather(root_inverse, 'row', axis=1, tiled=True)  9.03 us
  transfers between devices with their start and end apart: 5, of which 5 were waited for; matrix products, arithmetic and copies ran while one was open for 8% of the time, Pallas kernels for 0%

commit v1 on v0

--- a/solution.py
+++ b/solution.py
@@ -1,3 +1,4 @@
+import functools
 import jax
 import jax.numpy as jnp
 from jax import lax
@@ -5,6 +6,22 @@
 
 BLOCK = 128
 NSMAX = 12
+
+
+def compute_thing_all(sample, at_axis):
+    n_peers_all = jax.lax.axis_size("col")
+    met_up = [(hop_no - 1, hop_no) for hop_no in range(1, n_peers_all)] + [(n_peers_all - 1, 0)]
+    mat_out = sample
+    crops = [mat_out]
+    for _ in range(n_peers_all - 1):
+        mat_out = jax.lax.ppermute(mat_out, "col", met_up)
+        crops += [mat_out]
+    arr_now = jnp.concatenate([*reversed(crops)], at_axis)
+    part_now = jax.lax.axis_index("col")
+    return jnp.roll(arr_now, (part_now + 1) * mat_out.shape[at_axis], at_axis)
+
+
+loops_place = functools.partial(compute_thing_all, at_axis=1)
 
 
 def body(root_inverse, lower_panels, struct_blocks, struct_count, diag_inverse):
@@ -19,7 +36,7 @@
     def solve_group(lower_group, block_lists, block_counts, inverse_group):
         group_size = lower_group.shape[0]
         cols_here = lower_group.shape[2]
-        gathered = lax.all_gather(lower_group, "col", axis=1, tiled=True)
+        gathered = loops_place(lower_group)
         packed_total = gathered.shape[1]
         full_mask = jnp.arange(packed_total)[None, :] // BLOCK < block_counts[:, None]
         gathered = gathered * full_mask[:, :, None].astype(jnp.bfloat16)

time: 270 us -> 261 us (0.967)
  waiting for transfers between devices: 228 us -> 218 us
  starting transfers between devices: 0.19 us -> 3.2 us
    ppermute x0 -> x7, waiting for transfers between devices: none -> 78.1 us  [compute_thing_all(): mat_out = jax.lax.ppermute(mat_out, 'col', met_up)]
    all_gather x1 -> x0, waiting for transfers between devices: 61.3 us -> none  [solve_group(): gathered = lax.all_gather(lower_group, 'col', axis=1, tiled=True)]
    all_gather x1, waiting for transfers between devices: 9.62 us -> 0.01 us  [solve_group(): full_cols = lax.all_gather(lower_group, 'row', axis=2, tiled=True)]
    all_gather x1, waiting for transfers between devices: 9.03 us -> 0.01 us  [body(): root_panel = lax.all_gather(root_inverse, 'row', axis=1, tiled=True)]
    reduce_scatter x1, waiting for transfers between devices: 78.3 us -> 71.3 us  [solve_group(): lax.psum_scatter(selected.astype(jnp.bfloat16), 'col', scatter_dimension=...]
    ppermute x0 -> x7, starting transfers between devices: none -> 3.04 us  [compute_thing_all(): mat_out = jax.lax.ppermute(mat_out, 'col', met_up)]
  transfers between devices with their start and end apart: 5 -> 11, of which waited for: 5 -> 9; matrix products, arithmetic and copies ran while one was open for 8% -> 8% of each run, Pallas kernels for 0% -> 0%
where the time goes in v1:
time: 261 us
  waiting for transfers between devices  218 us (84%)
  matrix products  14 us (5%)
  between operations  14 us (5%)
  local copies, waits for them, and re-layouts  6.91 us (3%)
  other arithmetic  5.38 us (2%)
  starting transfers between devices  3.2 us (1%)
    ppermute x7, waiting for transfers between devices, compute_thing_all(): mat_out = jax.lax.ppermute(mat_out, 'col', met_up)  78.1 us
    reduce_scatter x1, waiting for transfers between devices, solve_group(): lax.psum_scatter(selected.astype(jnp.bfloat16), 'col', scatter_dimension=...  71.3 us
    reduce_scatter x1, waiting for transfers between devices, solve_group(): lax.psum_scatter(schur_terms.astype(jnp.bfloat16), 'col', scatter_dimensi...  68.1 us
  transfers between devices with their start and end apart: 11, of which 9 were waited for; matrix products, arithmetic and copies ran while one was open for 8% of the time, Pallas kernels for 0%

profile of v1, /device:TPU:0, one launch (start us, length us, event | category | flops | bytes accessed | tf_op | source)
XLA Modules:
  0.0 261.1 jit_solution(9844098853699714822)
XLA Ops:
  7.2 0.0 copy-start
  7.2 0.0 all-gather.3.cloned.1.call-start
  7.2 3.0 %collective-permute-start = (bf16[4,192,256]{2,1,0:T(8,128)(2,1)}, bf16[4,192,256]{2,1,0:T(8,128)(2,1)S(1)}, u32[]{:S(2)}, u32[]{:S(2)}) collective-permute-start(bf16[4,192,256]{2,1,0:T(8,128)(2,1)} %param.6), channel_id=1, source_target_pairs={{0,1},{1,2},{2,3},{3,4},{4,5},{5,6},{6,7},{7,0},{8,9},{9,10},{10,1... | collective-permute-start | bytes 1179656 | tf_op jit(solution)/shard_map/while/body/eval_jaxpr/ppermute | solution.py:17
  10.2 0.0 all-gather.3.cloned.1.call-update
  10.3 0.0 all-gather.5.cloned.1.call-start
  10.3 12.3 %collective-permute-done = bf16[4,192,256]{2,1,0:T(8,128)(2,1)S(1)} collective-permute-done((bf16[4,192,256]{2,1,0:T(8,128)(2,1)}, bf16[4,192,256]{2,1,0:T(8,128)(2,1)S(1)}, u32[]{:S(2)}, u32[]{:S(2)}) %collective-permute-start) | collective-permute-done | bytes 393248 | tf_op jit(solution)/shard_map/while/body/eval_jaxpr/ppermute | solution.py:17
  22.6 0.0 collective-permute-start.1
  22.6 13.0 %collective-permute-done.1 = bf16[4,192,256]{2,1,0:T(8,128)(2,1)S(1)} collective-permute-done((bf16[4,192,256]{2,1,0:T(8,128)(2,1)S(1)}, bf16[4,192,256]{2,1,0:T(8,128)(2,1)S(1)}, u32[]{:S(2)}, u32[]{:S(2)}) %collective-permute-start.1) | collective-permute-done | bytes 393248 | tf_op jit(solution)/shard_map/while/body/eval_jaxpr/ppermute | solution.py:17
  35.6 0.0 collective-permute-start.2
  35.6 12.1 %collective-permute-done.2 = bf16[4,192,256]{2,1,0:T(8,128)(2,1)S(1)} collective-permute-done((bf16[4,192,256]{2,1,0:T(8,128)(2,1)S(1)}, bf16[4,192,256]{2,1,0:T(8,128)(2,1)S(1)}, u32[]{:S(2)}, u32[]{:S(2)}) %collective-permute-start.2) | collective-permute-done | bytes 393248 | tf_op jit(solution)/shard_map/while/body/eval_jaxpr/ppermute | solution.py:17
  47.7 0.0 collective-permute-start.3
  47.7 11.3 %collective-permute-done.3 = bf16[4,192,256]{2,1,0:T(8,128)(2,1)S(1)} collective-permute-done((bf16[4,192,256]{2,1,0:T(8,128)(2,1)S(1)}, bf16[4,192,256]{2,1,0:T(8,128)(2,1)S(1)}, u32[]{:S(2)}, u32[]{:S(2)}) %collective-permute-start.3) | collective-permute-done | bytes 393248 | tf_op jit(solution)/shard_map/while/body/eval_jaxpr/ppermute | solution.py:17
  59.0 0.0 collective-permute-start.4
  59.0 0.0 all-gather.5.cloned.1.call-update
  59.0 0.0 reduce-scatter.3.cloned.1.call-start
  59.1 10.4 %collective-permute-done.4 = bf16[4,192,256]{2,1,0:T(8,128)(2,1)S(1)} collective-permute-done((bf16[4,192,256]{2,1,0:T(8,128)(2,1)S(1)}, bf16[4,192,256]{2,1,0:T(8,128)(2,1)S(1)}, u32[]{:S(2)}, u32[]{:S(2)}) %collective-permute-start.4) | collective-permute-done | bytes 393248 | tf_op jit(solution)/shard_map/while/body/eval_jaxpr/ppermute | solution.py:17
  69.4 0.0 collective-permute-start.5
  69.4 0.7 iota_compare_fusion.1
  70.2 0.7 fusion.9
  70.9 9.4 %collective-permute-done.5 = bf16[4,192,256]{2,1,0:T(8,128)(2,1)S(1)} collective-permute-done((bf16[4,192,256]{2,1,0:T(8,128)(2,1)S(1)}, bf16[4,192,256]{2,1,0:T(8,128)(2,1)S(1)}, u32[]{:S(2)}, u32[]{:S(2)}) %collective-permute-start.5) | collective-permute-done | bytes 393248 | tf_op jit(solution)/shard_map/while/body/eval_jaxpr/ppermute | solution.py:17
  80.2 0.0 collective-permute-start.6
  80.2 0.7 compare_convert_fusion
  81.0 9.7 %collective-permute-done.6 = bf16[4,192,256]{2,1,0:T(8,128)(2,1)S(1)} collective-permute-done((bf16[4,192,256]{2,1,0:T(8,128)(2,1)S(1)}, bf16[4,192,256]{2,1,0:T(8,128)(2,1)S(1)}, u32[]{:S(2)}, u32[]{:S(2)}) %collective-permute-start.6) | collective-permute-done | bytes 393248 | tf_op jit(solution)/shard_map/while/body/eval_jaxpr/ppermute | solution.py:17
  90.9 0.0 copy-done
  91.0 0.0 copy-start.2
  91.3 1.3 dynamic-slice_multiply_fusion
  92.6 0.0 copy-done.2
  92.6 2.0 fusion.2
  94.6 3.5 %copy.10 = bf16[4,16,128,256]{3,2,1,0:T(8,128)(2,1)} copy(bf16[4,16,128,256]{3,1,2,0:T(8,128)(2,1)S(1)} %fusion.2) | data formatting | bytes 8388608 | tf_op jit(solution)/shard_map/while/body/eval_jaxpr/convert_element_type | solution.py:53
  98.2 0.0 all-gather.3.cloned.1.call-done
  98.2 3.8 %convolution_negate_fusion = f32[4,256,256]{1,2,0:T(8,128)S(1)} fusion(bf16[4,2048,256]{2,1,0:T(8,128)(2,1)} %bitcast.23, bf16[256,2048]{1,0:T(8,128)(2,1)} %all-gather.3.cloned.1.call-done), kind=kOutput, calls=%fused_computation.7 | convolution fusion | flops 1074003968 | bytes 6291456 | tf_op jit(solution)/shard_map/while/body/eval_jaxpr/rw,gwc->grc/dot_general | solution.py:54
  102.0 4.4 %convolution_convert_fusion = bf16[4,12,128,256]{3,1,2,0:T(8,128)(2,1)S(1)} fusion(f32[4,2,128,256]{3,2,1,0:T(8,128)S(1)} %bitcast.24, pred[4,16,12]{2,1,0:T(8,128)(4,1)S(1)} %fusion.9, s32[]{:T(128)S(6)} %select_n.42), kind=kOutput, calls=%fused_computation.4 | convolution fusion | flops 39321600 | bytes 4196356 | tf_op jit(solution)/shard_map/while/body/eval_jaxpr/gjk,gjic->gkic/dot_general | solution.py:62
  106.4 0.0 copy-start.3
  106.4 2.9 %copy.12 = bf16[4,12,128,256]{3,2,1,0:T(8,128)(2,1)} copy(bf16[4,12,128,256]{3,1,2,0:T(8,128)(2,1)S(1)} %convolution_convert_fusion) | data formatting | bytes 6291456 | tf_op jit(solution)/shard_map/while/body/eval_jaxpr/convert_element_type | solution.py:71
  109.3 0.0 copy-start.1
  109.3 0.0 reduce-scatter.3.cloned.1.call-update
  109.3 0.0 reduce-scatter.5.cloned.1.call-start
  109.4 0.0 copy-done.3
  109.4 0.1 compare_convert_fusion.1
  109.5 0.0 all-gather.5.cloned.1.call-done
  109.5 71.3 %reduce-scatter.3.cloned.1.call-done = bf16[4,192,256]{2,1,0:T(8,128)(2,1)} async-done(((bf16[4,1536,256]{2,1,0:T(8,128)(2,1)}), bf16[4,192,256]{2,1,0:T(8,128)(2,1)}) %reduce-scatter.3.cloned.1.call-update) | async-done | bytes 393232 | tf_op jit(solution)/shard_map/while/body/eval_jaxpr/reduce_scatter | solution.py:70
  180.7 3.9 %convolution_convert_fusion.1 = bf16[4,1024,256]{2,1,0:T(8,128)(2,1)} fusion(bf16[4,192,256]{2,1,0:T(8,128)(2,1)} %reduce-scatter.3.cloned.1.call-done, bf16[4,192,1024]{2,1,0:T(8,128)(2,1)} %all-gather.5.cloned.1.call-done, bf16[4,192]{1,0:T(4,128)(2,1)S(1)} %compare_convert_fusion.1), kind=kOutput, calls=%fused_computation.5 | convolution fusion | flops 404488192 | bytes 4064768 | tf_op jit(solution)/shard_map/while/body/eval_jaxpr/gka,gkc->gac/dot_general | solution.py:75
  184.6 0.0 reduce-scatter.5.cloned.1.call-update
  184.6 68.1 %reduce-scatter.5.cloned.1.call-done = bf16[4,128,256]{2,1,0:T(8,128)(2,1)} async-done(((bf16[4,1024,256]{2,1,0:T(8,128)(2,1)}), bf16[4,128,256]{2,1,0:T(8,128)(2,1)}) %reduce-scatter.5.cloned.1.call-update) | async-done | bytes 262160 | tf_op jit(solution)/shard_map/while/body/eval_jaxpr/reduce_scatter | solution.py:78
  252.7 0.0 copy-done.1
  252.7 1.8 convert_subtract_fusion
  (18 shorter events, 0.5 us)
Async XLA Ops:
  7.2 83.8 %copy-start = (bf16[4,192,256]{2,1,0:T(8,128)(2,1)S(1)}, bf16[4,192,256]{2,1,0:T(8,128)(2,1)}, u32[]{:S(2)}) copy-start(bf16[4,192,256]{2,1,0:T(8,128)(2,1)} %param.6) | copy-start | bytes 1179652
  7.2 91.0 %all-gather.3.cloned.1.call-start = ((), (), s32[]{:S(2)}) async-start(), calls=%async_computation.2 | async-start | bytes 1310720 | tf_op jit(solution)/shard_map/all_gather | solution.py:29
  7.2 15.4 %collective-permute-start = (bf16[4,192,256]{2,1,0:T(8,128)(2,1)}, bf16[4,192,256]{2,1,0:T(8,128)(2,1)S(1)}, u32[]{:S(2)}, u32[]{:S(2)}) collective-permute-start(bf16[4,192,256]{2,1,0:T(8,128)(2,1)} %param.6), channel_id=1, source_target_pairs={{0,1},{1,2},{2,3},{3,4},{4,5},{5,6},{6,7},{7,0},{8,9},{9,10},{10,1... | collective-permute-start | bytes 1179656 | tf_op jit(solution)/shard_map/while/body/eval_jaxpr/ppermute | solution.py:17
  10.3 99.2 %all-gather.5.cloned.1.call-start = ((), (), s32[]{:S(2)}) async-start(), calls=%async_computation.4 | async-start | bytes 1966080 | tf_op jit(solution)/shard_map/while/body/eval_jaxpr/all_gather | solution.py:73
  22.6 13.0 %collective-permute-start.1 = (bf16[4,192,256]{2,1,0:T(8,128)(2,1)S(1)}, bf16[4,192,256]{2,1,0:T(8,128)(2,1)S(1)}, u32[]{:S(2)}, u32[]{:S(2)}) collective-permute-start(bf16[4,192,256]{2,1,0:T(8,128)(2,1)S(1)} %collective-permute-done), channel_id=1, source_target_pairs={{0,1},{1,2},{2,3},{3,4},{4,5},{5,6},{6,7},{7,0},{8,9},{9,10},{10,1... | collective-permute-start | bytes 1179656 | tf_op jit(solution)/shard_map/while/body/eval_jaxpr/ppermute | solution.py:17
  35.6 12.1 %collective-permute-start.2 = (bf16[4,192,256]{2,1,0:T(8,128)(2,1)S(1)}, bf16[4,192,256]{2,1,0:T(8,128)(2,1)S(1)}, u32[]{:S(2)}, u32[]{:S(2)}) collective-permute-start(bf16[4,192,256]{2,1,0:T(8,128)(2,1)S(1)} %collective-permute-done.1), channel_id=1, source_target_pairs={{0,1},{1,2},{2,3},{3,4},{4,5},{5,6},{6,7},{7,0},{8,9},{9,10},{10,1... | collective-permute-start | bytes 1179656 | tf_op jit(solution)/shard_map/while/body/eval_jaxpr/ppermute | solution.py:17
  47.7 11.3 %collective-permute-start.3 = (bf16[4,192,256]{2,1,0:T(8,128)(2,1)S(1)}, bf16[4,192,256]{2,1,0:T(8,128)(2,1)S(1)}, u32[]{:S(2)}, u32[]{:S(2)}) collective-permute-start(bf16[4,192,256]{2,1,0:T(8,128)(2,1)S(1)} %collective-permute-done.2), channel_id=1, source_target_pairs={{0,1},{1,2},{2,3},{3,4},{4,5},{5,6},{6,7},{7,0},{8,9},{9,10},{10,1... | collective-permute-start | bytes 1179656 | tf_op jit(solution)/shard_map/while/body/eval_jaxpr/ppermute | solution.py:17
  59.0 10.5 %collective-permute-start.4 = (bf16[4,192,256]{2,1,0:T(8,128)(2,1)S(1)}, bf16[4,192,256]{2,1,0:T(8,128)(2,1)S(1)}, u32[]{:S(2)}, u32[]{:S(2)}) collective-permute-start(bf16[4,192,256]{2,1,0:T(8,128)(2,1)S(1)} %collective-permute-done.3), channel_id=1, source_target_pairs={{0,1},{1,2},{2,3},{3,4},{4,5},{5,6},{6,7},{7,0},{8,9},{9,10},{10,1... | collective-permute-start | bytes 1179656 | tf_op jit(solution)/shard_map/while/body/eval_jaxpr/ppermute | solution.py:17
  59.0 121.8 %reduce-scatter.3.cloned.1.call-start = ((), (), s32[]{:S(2)}) async-start(), calls=%async_computation.3 | async-start | bytes 3538944 | tf_op jit(solution)/shard_map/while/body/eval_jaxpr/reduce_scatter | solution.py:70
  69.4 10.8 %collective-permute-start.5 = (bf16[4,192,256]{2,1,0:T(8,128)(2,1)S(1)}, bf16[4,192,256]{2,1,0:T(8,128)(2,1)S(1)}, u32[]{:S(2)}, u32[]{:S(2)}) collective-permute-start(bf16[4,192,256]{2,1,0:T(8,128)(2,1)S(1)} %collective-permute-done.4), channel_id=1, source_target_pairs={{0,1},{1,2},{2,3},{3,4},{4,5},{5,6},{6,7},{7,0},{8,9},{9,10},{10,1... | collective-permute-start | bytes 1179656 | tf_op jit(solution)/shard_map/while/body/eval_jaxpr/ppermute | solution.py:17
  80.2 10.5 %collective-permute-start.6 = (bf16[4,192,256]{2,1,0:T(8,128)(2,1)S(1)}, bf16[4,192,256]{2,1,0:T(8,128)(2,1)S(1)}, u32[]{:S(2)}, u32[]{:S(2)}) collective-permute-start(bf16[4,192,256]{2,1,0:T(8,128)(2,1)S(1)} %collective-permute-done.5), channel_id=1, source_target_pairs={{0,1},{1,2},{2,3},{3,4},{4,5},{5,6},{6,7},{7,0},{8,9},{9,10},{10,1... | collective-permute-start | bytes 1179656 | tf_op jit(solution)/shard_map/while/body/eval_jaxpr/ppermute | solution.py:17
  91.0 1.6 copy-start.2
  106.4 3.0 %copy-start.3 = (s32[4]{0:T(128)S(1)}, s32[4]{0:T(128)}, u32[]{:S(2)}) copy-start(s32[4]{0:T(128)} %param.8) | copy-start | bytes 52
  109.3 143.4 %copy-start.1 = (f32[4,128,256]{2,1,0:T(8,128)S(1)}, f32[4,128,256]{2,1,0:T(8,128)}, u32[]{:S(2)}) copy-start(f32[4,128,256]{2,1,0:T(8,128)} %param.9) | copy-start | bytes 1572868
  109.3 143.4 %reduce-scatter.5.cloned.1.call-start = ((), (), s32[]{:S(2)}) async-start(), calls=%async_computation.5 | async-start | bytes 2359296 | tf_op jit(solution)/shard_map/while/body/eval_jaxpr/reduce_scatter | solution.py:78
Sparse Core Ops, SparseCore 0:
  10.4 18.5 all-gather.2
  59.1 20.6 all-gather.4
  109.4 71.2 reduce-scatter.2
  184.8 67.9 reduce-scatter.4
